TPU v7x, 512 devices: a 8x2x16 block of a 8x16x16 slice. The times are simulated.
512 devices in a mesh: rep: 2 (over y), blk: 128 (over z, x), head: 2 (over core).
Axes of the slice: x: 8, y: 2, z: 16, core: 2. Of those that a mesh axis runs over, the one named last changes fastest.
The devices are a block of a 8x16x16 slice.
Arguments:
- queries: bfloat16 [2, 8192, 8192], P('rep', 'blk', 'head'), parts along dimension 0, may hold values from -200 to 200
- keys: bfloat16 [2, 8192, 512], P('rep', 'blk', 'head'), parts along dimension 0, may hold values from -6 to 6
- values: bfloat16 [2, 8192, 512], P('rep', 'blk', 'head'), parts along dimension 0, may hold values from -6 to 6
- prompt_length: int32 [2], P('rep'), parts along dimension 0, may hold values from 4096 to 8192
- span_order: int32 [512], P('rep'), parts along dimension 0, may hold values from 0 to 255, as said below
Outputs:
- attended: bfloat16 [2, 8192, 8192], P('rep', 'blk', 'head'), parts along dimension 0
There are 2 independent parts, one for each index of `rep`. A program takes and returns all parts, laid end to end along the dimension named above; each array names one. Nothing has to cross between parts.
Inputs may be any that keep to these rules, and one draw needn't show every extreme that they name: `span_order`: each of the 256 span numbers stands in exactly one slot.
All inputs are finite; a program needn't handle non-finite values.
Results may differ from a plain program's by a relative error of at most 0.0065.
Values may be sent and summed in bfloat16 or wider, within the bound.
No kernel may reach another device: no remote copies, remote signals or barrier semaphores. Data moves between devices by JAX's collectives and lax.ppermute only.
A program may use at most 64 MiB of HBM per device.

v0:
```python
import jax
import jax.numpy as jnp
from jax import lax
from jax.sharding import Mesh
from jax.sharding import PartitionSpec as P

HEAD_WIDTH = 128
BLK = ("blk_0", "blk_1")
NEG_FILL = -1e30


def laid_out(pieces, dim):
    pieces = jnp.moveaxis(pieces, 0, dim)
    shape = pieces.shape
    return pieces.reshape(*shape[:dim], shape[dim] * shape[dim + 1], *shape[dim + 2 :])


def stacked_from(value, axes, sequence):
    pieces = value[None]
    for k in sequence:
        pieces = lax.all_gather(pieces, axes[k], axis=0, tiled=True)
    carried = [lax.axis_size(axes[k]) for k in reversed(sequence)]
    pieces = pieces.reshape(*carried, *value.shape)
    turned = sorted(range(len(sequence)), key=lambda place: sequence[len(sequence) - 1 - place])
    return pieces.transpose(*turned, *range(len(sequence), pieces.ndim)).reshape(-1, *value.shape)


def whole_of(value, axes, sequence, dim):
    return laid_out(stacked_from(value, axes, sequence), dim)


def shards(queries, keys, values, prompt_length, span_order):
    mine = lax.axis_index(BLK)
    prompts = queries.shape[0]
    tok_rows = queries.shape[1]
    span = tok_rows // 2
    local_heads = keys.shape[2] // HEAD_WIDTH
    group = queries.shape[2] // (local_heads * HEAD_WIDTH)
    offsets = jnp.arange(span, dtype=jnp.int32)
    all_pos = (span_order[:, None] * span + offsets[None, :]).reshape(-1)
    my_pos = lax.dynamic_slice_in_dim(all_pos, mine * tok_rows, tok_rows)
    row_pos = jnp.tile(my_pos, group)
    q_cols = (
        queries.reshape(prompts, tok_rows, local_heads, group, HEAD_WIDTH)
        .transpose(0, 2, 4, 3, 1)
        .reshape(prompts, local_heads, HEAD_WIDTH, group * tok_rows)
    )
    scale = HEAD_WIDTH ** (-0.5)

    def attend(carry, key_rows, value_rows, key_pos):
        best, total, accum = carry
        count = key_rows.shape[1]
        key_four = key_rows.reshape(prompts, count, local_heads, HEAD_WIDTH)
        value_four = value_rows.reshape(prompts, count, local_heads, HEAD_WIDTH)
        scores = (
            jnp.einsum("skhd,shdr->shkr", key_four, q_cols, preferred_element_type=jnp.float32)
            * scale
        )
        allowed = (key_pos[None, :, None] <= row_pos[None, None, :]) & (
            key_pos[None, :, None] < prompt_length[:, None, None]
        )
        scores = jnp.where(allowed[:, None], scores, NEG_FILL)
        fresh = jnp.maximum(best, jnp.max(scores, axis=2))
        weights = jnp.where(allowed[:, None], jnp.exp(scores - fresh[:, :, None, :]), 0.0)
        factor = jnp.exp(best - fresh)
        total = total * factor + jnp.sum(weights, axis=2)
        mixed = jnp.einsum(
            "shkr,skhd->shrd",
            weights.astype(jnp.bfloat16),
            value_four,
            preferred_element_type=jnp.float32,
        )
        accum = accum * factor[..., None] + mixed
        return (fresh, total, accum)

    def visit(carry, key_rows, value_rows, key_pos):
        return attend(carry, key_rows, value_rows, key_pos)

    def fold_piece(carry, pieces):
        key_rows, value_rows = pieces
        rows = key_rows.shape[1]
        size = max((d for d in range(1, min(rows, 256) + 1) if rows % d == 0))
        steps = rows // size
        if steps == 1:
            return visit(carry, key_rows, value_rows, all_pos)

        def one_block(index, state):
            begin = (index * size).astype(jnp.int32)
            return visit(
                state,
                lax.dynamic_slice_in_dim(key_rows, begin, size, 1),
                lax.dynamic_slice_in_dim(value_rows, begin, size, 1),
                lax.dynamic_slice_in_dim(all_pos, begin, size),
            )

        return lax.fori_loop(0, steps, one_block, carry)

    width = group * tok_rows
    init = (
        jnp.full((prompts, local_heads, width), NEG_FILL, jnp.float32),
        jnp.zeros((prompts, local_heads, width), jnp.float32),
        jnp.zeros((prompts, local_heads, width, HEAD_WIDTH), jnp.float32),
    )
    carry = fold_piece(init, (whole_of(keys, BLK, (0, 1), 1), whole_of(values, BLK, (0, 1), 1)))
    best, total, accum = carry
    normed = accum / total[..., None]
    joined_heads = (
        normed.reshape(prompts, local_heads, group, tok_rows, HEAD_WIDTH)
        .transpose(0, 3, 1, 2, 4)
        .reshape(prompts, tok_rows, local_heads * group * HEAD_WIDTH)
    )
    joined_heads = jnp.where(
        (my_pos[None, :] < prompt_length[:, None])[:, :, None], joined_heads, 0.0
    )
    return joined_heads.astype(jnp.bfloat16)


def solution(mesh):
    split = Mesh(
        mesh.devices.reshape(mesh.shape["rep"], 16, 8, mesh.shape["head"]),
        ("rep", "blk_0", "blk_1", "head"),
    )
    in_specs = (
        P("rep", BLK, "head"),
        P("rep", BLK, "head"),
        P("rep", BLK, "head"),
        P("rep"),
        P("rep"),
    )
    out_specs = P("rep", BLK, "head")
    return jax.shard_map(
        shards, mesh=split, in_specs=in_specs, out_specs=out_specs, check_vma=False
    )
```

profile of v0, /device:TPU:65, one launch (start us, length us, event | category | flops | bytes accessed | tf_op | source)
XLA Modules:
  0.0 430.8 jit_solution(16120057133728882408)
XLA Ops:
  6.6 67.5 %all-gather = bf16[16,64,256]{2,1,0:T(8,128)(2,1)} all-gather(bf16[1,64,256]{2,1,0:T(8,128)(2,1)} %param.8), channel_id=2, replica_groups=mesh['rep'=2,'blk_0'=16,'blk_1'=8,'head'=2] {'blk_0'}, dimensions={0}, use_global_device_ids=true | all-gather | bytes 557056 | tf_op jit(solution)/shard_map/all_gather | solution.py:21
  74.2 25.9 %all-gather.2 = bf16[16,64,256]{2,1,0:T(8,128)(2,1)} all-gather(bf16[1,64,256]{2,1,0:T(8,128)(2,1)} %param.9), channel_id=4, replica_groups=mesh['rep'=2,'blk_0'=16,'blk_1'=8,'head'=2] {'blk_0'}, dimensions={0}, use_global_device_ids=true | all-gather | bytes 557056 | tf_op jit(solution)/shard_map/all_gather | solution.py:21
  101.6 33.6 %all-gather.7.cloned.1.call-done = bf16[128,64,256]{2,1,0:T(8,128)(2,1)} async-done(((bf16[16,64,256]{2,1,0:T(8,128)(2,1)}), bf16[128,64,256]{2,1,0:T(8,128)(2,1)}) %all-gather.7.cloned.1.call-update) | async-done | bytes 4194320 | tf_op jit(solution)/shard_map/all_gather | solution.py:21
  135.2 4.7 %copy.39 = bf16[16,8,1,64,256]{4,3,1,0,2:T(8,128)(2,1)} copy(bf16[16,8,1,64,256]{4,3,0,1,2:T(8,128)(2,1)} %bitcast.69) | data formatting | bytes 8388608 | tf_op jit(solution)/shard_map/transpose | solution.py:25
  139.9 57.4 %all-gather.9.cloned.1.call-done = bf16[128,64,256]{2,1,0:T(8,128)(2,1)} async-done(((bf16[16,64,256]{2,1,0:T(8,128)(2,1)}), bf16[128,64,256]{2,1,0:T(8,128)(2,1)}) %all-gather.9.cloned.1.call-update) | async-done | bytes 4194320 | tf_op jit(solution)/shard_map/all_gather | solution.py:21
  197.4 4.8 %copy.41 = bf16[16,8,1,64,256]{4,3,1,0,2:T(8,128)(2,1)} copy(bf16[16,8,1,64,256]{4,3,0,1,2:T(8,128)(2,1)} %bitcast.70) | data formatting | bytes 8388608 | tf_op jit(solution)/shard_map/transpose | solution.py:25
  202.1 218.6 %while.18 = (s32[]{:T(128)}, f32[1,2,1024]{2,1,0:T(2,128)S(1)}, f32[1,2,1024]{2,1,0:T(2,128)S(1)}, f32[1,2,1024,128]{3,2,1,0:T(8,128)}, s32[8192]{0:T(1024)S(1)}...) while((s32[]{:T(128)}, f32[1,2,1024]{2,1,0:T(2,128)S(1)}, ...), condition=%wide.region_3.4_spmd.clone, body=%wide.region_0.3_spmd.clone.sunk | while | flops 276574464 | bytes 11423691 | solution.py:96
  210.7 3.3 fusion.33
  217.6 3.3 fusion.33
  224.5 3.3 fusion.33
  231.4 3.3 fusion.33
  238.2 3.3 fusion.33
  245.1 3.3 fusion.33
  252.0 3.3 fusion.33
  258.8 3.3 fusion.33
  265.7 3.3 fusion.33
  272.6 3.3 fusion.33
  279.5 3.3 fusion.33
  286.3 3.3 fusion.33
  293.2 3.3 fusion.33
  306.9 3.3 fusion.33
  313.8 3.3 fusion.33
  320.7 3.3 fusion.33
  327.6 3.3 fusion.33
  (421 shorter events, 164.3 us)
Async XLA Ops:
  6.5 93.6 %copy-start.1 = (s32[256]{0:T(256)S(1)}, s32[256]{0:T(256)}, u32[]{:S(2)}) copy-start(s32[256]{0:T(256)} %param.11) | copy-start | bytes 3076
  6.5 94.5 %copy-start = (bf16[1,64,4096]{2,1,0:T(8,128)(2,1)S(1)}, bf16[1,64,4096]{2,1,0:T(8,128)(2,1)}, u32[]{:S(2)}) copy-start(bf16[1,64,4096]{2,1,0:T(8,128)(2,1)} %param.7) | copy-start | bytes 1572868
  6.6 128.7 %all-gather.7.cloned.1.call-start = ((), (), s32[]{:S(2)}) async-start(), calls=%async_computation | async-start | bytes 4718592 | tf_op jit(solution)/shard_map/all_gather | solution.py:21
  74.1 123.3 %all-gather.9.cloned.1.call-start = ((), (), s32[]{:S(2)}) async-start(), calls=%async_computation.1 | async-start | bytes 4718592 | tf_op jit(solution)/shard_map/all_gather | solution.py:21
Sparse Core Ops, SparseCore 0:
  74.2 60.9 all-gather.6
  137.3 60.0 all-gather.8
where the time goes:
time: 433 us; the launch traced here: 431 us
  matrix products  125 us (29%)
  blocking collectives  93.4 us (22%)
  waiting for transfers between devices  91.1 us (21%)
  other arithmetic  53.3 us (12%)
  local copies, waits for them, and re-layouts  51.2 us (12%)
  between operations  14.2 us (3%)
    dot_general x32, matrix products, attend(): jnp.einsum('shkr,skhd->shrd', weights.astype(jnp.bfloat16), value_four, p...  104 us
    all_gather x2, blocking collectives, stacked_from(): pieces = lax.all_gather(pieces, axes[k], axis=0, tiled=True)  93.4 us
    all_gather x2, waiting for transfers between devices, stacked_from(): pieces = lax.all_gather(pieces, axes[k], axis=0, tiled=True)  91 us
    dynamic_slice x64, local copies, waits for them, and re-layouts, one_block(): lax.dynamic_slice_in_dim(value_rows, begin, size, 1)  34.9 us
    lt x32, other arithmetic, attend(): key_pos[None, :, None] < prompt_length[:, None, None]  23.3 us
    dot_general x32, matrix products, attend(): jnp.einsum('skhd,shdr->shkr', key_four, q_cols, preferred_element_type=jn...  20.9 us
    reduce_sum x32, other arithmetic, attend(): total = total * factor + jnp.sum(weights, axis=2)  18.2 us
    transpose x2, local copies, waits for them, and re-layouts, stacked_from(): pieces.transpose(*turned, *range(len(sequence), pieces.ndim))  9.46 us
  transfers between devices with their start and end apart: 2, of which 2 were waited for; matrix products, arithmetic and copies ran while one was open for 1% of the time, Pallas kernels for 0%

commit v1 on v0

--- a/solution.py
+++ b/solution.py
@@ -18,7 +18,9 @@
 def stacked_from(value, axes, sequence):
     pieces = value[None]
     for k in sequence:
-        pieces = lax.all_gather(pieces, axes[k], axis=0, tiled=True)
+        pieces = jnp.concatenate(
+            lax.all_to_all(jnp.stack([pieces] * lax.axis_size(axes[k])), axes[k], 0, 0), axis=0
+        )
     carried = [lax.axis_size(axes[k]) for k in reversed(sequence)]
     pieces = pieces.reshape(*carried, *value.shape)
     turned = sorted(range(len(sequence)), key=lambda place: sequence[len(sequence) - 1 - place])

time: 433 us -> 531 us (1.23)
  the two profiles are of different devices: /device:TPU:65 before, /device:TPU:320 now
where the time goes in v1:
time: 531 us; the launch traced here: 529 us
  blocking collectives  204 us (38%)
  matrix products  123 us (23%)
  waiting for transfers between devices  84.4 us (16%)
  local copies, waits for them, and re-layouts  55.8 us (11%)
  other arithmetic  53.3 us (10%)
    all_to_all x3, blocking collectives, stacked_from(): lax.all_to_all(jnp.stack([pieces] * lax.axis_size(axes[k])), axes[k], 0, 0)  204 us
    dot_general x32, matrix products, attend(): jnp.einsum('shkr,skhd->shrd', weights.astype(jnp.bfloat16), value_four, p...  102 us
    all_to_all x1, waiting for transfers between devices, stacked_from(): lax.all_to_all(jnp.stack([pieces] * lax.axis_size(axes[k])), axes[k], 0, 0)  84.4 us
    dynamic_slice x64, local copies, waits for them, and re-layouts, one_block(): lax.dynamic_slice_in_dim(value_rows, begin, size, 1)  34.9 us
    lt x32, other arithmetic, attend(): key_pos[None, :, None] < prompt_length[:, None, None]  23.3 us
    dot_general x32, matrix products, attend(): jnp.einsum('skhd,shdr->shkr', key_four, q_cols, preferred_element_type=jn...  20.7 us
    reduce_sum x32, other arithmetic, attend(): total = total * factor + jnp.sum(weights, axis=2)  18.2 us
  transfers between devices with their start and end apart: 1, of which 1 were waited for; matrix products, arithmetic and copies ran while one was open for 1% of the time, Pallas kernels for 0%

profile of v1, /device:TPU:320, one launch (start us, length us, event | category | flops | bytes accessed | tf_op | source)
XLA Modules:
  0.0 528.8 jit_solution(12692148792876400360)
XLA Ops:
  0.8 69.7 %all_to_all.20 = bf16[16,1,1,64,256]{4,3,2,1,0:T(8,128)(2,1)S(1)} all-to-all(bf16[16,1,1,64,256]{4,3,2,1,0:T(8,128)(2,1)S(1)} %stack.14), channel_id=1, replica_groups=mesh['rep'=2,'blk_0'=16,'blk_1'=8,'head'=2] {'blk_0'}, dimensions={0} | all-to-all | bytes 1048576 | tf_op jit(solution)/shard_map/all_to_all | solution.py:22
  71.3 35.3 %all_to_all.21 = bf16[16,1,1,64,256]{4,3,2,1,0:T(8,128)(2,1)S(1)} all-to-all(bf16[16,1,1,64,256]{4,3,2,1,0:T(8,128)(2,1)S(1)} %stack.12), channel_id=1, replica_groups=mesh['rep'=2,'blk_0'=16,'blk_1'=8,'head'=2] {'blk_0'}, dimensions={0} | all-to-all | bytes 1048576 | tf_op jit(solution)/shard_map/all_to_all | solution.py:22
  107.2 99.2 %all_to_all.22 = bf16[8,16,1,64,256]{4,3,1,2,0:T(8,128)(2,1)} all-to-all(bf16[8,16,1,64,256]{4,3,1,2,0:T(8,128)(2,1)S(1)} %stack.15), channel_id=1, replica_groups=mesh['rep'=2,'blk_0'=16,'blk_1'=8,'head'=2] {'blk_1'}, dimensions={0} | all-to-all | bytes 8388608 | tf_op jit(solution)/shard_map/all_to_all | solution.py:22
  208.9 4.9 all-to-all-start.1
  215.3 4.7 copy.29
  220.0 84.4 %all-to-all-done.1 = bf16[8,16,1,64,256]{4,3,1,2,0:T(8,128)(2,1)} async-done(((bf16[8,16,1,64,256]{4,3,1,2,0:T(8,128)(2,1)}), bf16[8,16,1,64,256]{4,3,1,2,0:T(8,128)(2,1)}, u32[]{:S(2)}, u32[]{:S(2)}) %all-to-all-start.1) | async-done | bytes 4194336 | tf_op jit(solution)/shard_map/all_to_all | solution.py:22
  304.5 4.7 copy.27
  309.2 216.5 %while.18 = (s32[]{:T(128)}, f32[1,2,1024]{2,1,0:T(2,128)S(1)}, f32[1,2,1024]{2,1,0:T(2,128)S(1)}, f32[1,2,1024,128]{3,2,1,0:T(8,128)}, s32[8192]{0:T(1024)S(1)}...) while((s32[]{:T(128)}, f32[1,2,1024]{2,1,0:T(2,128)S(1)}, ...), condition=%wide.region_3.4_spmd.clone, body=%wide.region_0.3_spmd.clone.sunk | while | flops 276574464 | bytes 11423691 | solution.py:98
  317.7 3.2 fusion.33
  324.5 3.2 fusion.33
  331.3 3.2 fusion.33
  338.1 3.2 fusion.33
  344.9 3.2 fusion.33
  351.7 3.2 fusion.33
  358.5 3.2 fusion.33
  365.4 3.2 fusion.33
  372.2 3.2 fusion.33
  379.0 3.2 fusion.33
  385.8 3.2 fusion.33
  392.6 3.2 fusion.33
  399.4 3.2 fusion.33
  406.2 3.2 fusion.33
  413.0 3.2 fusion.33
  419.8 3.2 fusion.33
  (422 shorter events, 170.9 us)
Async XLA Ops:
  208.9 5.0 copy-start.1
  208.9 5.8 %copy-start = (bf16[1,64,4096]{2,1,0:T(8,128)(2,1)S(1)}, bf16[1,64,4096]{2,1,0:T(8,128)(2,1)}, u32[]{:S(2)}) copy-start(bf16[1,64,4096]{2,1,0:T(8,128)(2,1)} %param.7) | copy-start | bytes 1572868
  208.9 95.6 %all-to-all-start.1 = ((bf16[8,16,1,64,256]{4,3,1,2,0:T(8,128)(2,1)}), bf16[8,16,1,64,256]{4,3,1,2,0:T(8,128)(2,1)}, u32[]{:S(2)}, u32[]{:S(2)}) async-start(bf16[8,16,1,64,256]{4,3,1,2,0:T(8,128)(2,1)} %stack.13), calls=%async_computation.1 | async-start | bytes 8388608 | tf_op jit(solution)/shard_map/all_to_all | solution.py:22
